TPU v7x, 32 devices: a whole 2x2x4 slice. The times are simulated.
32 devices in a mesh: rep: 2 (over x), shard: 16 (over z, y, core).
Axes of the slice: x: 2, y: 2, z: 4, core: 2. Of those that a mesh axis runs over, the one named last changes fastest.
Arguments:
- tokens: bfloat16 [4096, 2048], P(('rep', 'shard')), may hold values from -6 to 6
- segment_ids: int32 [4096], P(('rep', 'shard')), may hold values from -1 to 31, as said below
- cotangent: bfloat16 [4096, 2048], P(('rep', 'shard')), may hold values from -6 to 6
- w_qkv: bfloat16 [2048, 6144], P('shard'), may hold values from -0.125 to 0.125
- w_out: bfloat16 [2048, 2048], P('shard'), may hold values from -0.125 to 0.125
- w_gate_up: bfloat16 [2048, 16384], P('shard'), may hold values from -0.125 to 0.125
- w_down: bfloat16 [8192, 2048], P('shard'), may hold values from -0.0625 to 0.0625
- q_gain: bfloat16 [2048], P('shard'), may hold values from 0.5 to 1.5
- k_gain: bfloat16 [2048], P('shard'), may hold values from 0.5 to 1.5
- attn_gain: bfloat16 [2048], P('shard'), may hold values from 0.5 to 1.5
- mlp_gain: bfloat16 [2048], P('shard'), may hold values from 0.5 to 1.5
Outputs:
- output: bfloat16 [4096, 2048], P(('rep', 'shard'))
- grad_tokens: float32 [4096, 2048], P(('rep', 'shard'))
- grad_qkv: float32 [2048, 6144], P('shard')
- grad_out: float32 [2048, 2048], P('shard')
- grad_gate_up: float32 [2048, 16384], P('shard')
- grad_down: float32 [8192, 2048], P('shard')
- grad_q_gain: float32 [2048], P('shard')
- grad_k_gain: float32 [2048], P('shard')
- grad_attn_gain: float32 [2048], P('shard')
- grad_mlp_gain: float32 [2048], P('shard')
Inputs may be any that keep to these rules, and one draw needn't show every extreme that they name: `segment_ids`: within each block of 128 slots, live slots come first in runs of equal ids numbered upwards from 0 (one packed sequence each), each run starting at a slot whose index within the block is a multiple of 4, then padding slots with id -1; at least one block has no padding and starts a run at every multiple of 4.
All inputs are finite; a program needn't handle non-finite values.
Results may differ from a plain program's by a relative error of at most 0.02.
Values may be sent and summed in bfloat16 or wider, within the bound.
A program may use at most 384 MiB of HBM per device.

v0:
```python
import jax
import jax.numpy as jnp
from jax import lax
from jax.sharding import PartitionSpec as P

H = 16
EPSILON = 1e-06
THETA = 500000.0
BF = jnp.bfloat16
F32 = jnp.float32


def positions(seg):
    slots = lax.broadcasted_iota(jnp.int32, seg.shape, 1)
    starts = jnp.concatenate(
        [jnp.ones((seg.shape[0], 1), jnp.bool_), seg[:, 1:] != seg[:, :-1]], axis=1
    )
    first = lax.cummax(jnp.where(starts, slots, 0), axis=1)
    return slots - first


def rope_tables(seg, head_width):
    half_width = head_width // 2
    spots = positions(seg).astype(F32).reshape(-1)
    inverse = THETA ** (-(2.0 * jnp.arange(half_width, dtype=F32)) / head_width)
    angle = spots[:, None] * inverse[None, :]
    return (jnp.cos(angle), jnp.sin(angle))


def rotate(matrix, cosine, sine):
    half = matrix.shape[-1] // 2
    a, b = (matrix[..., :half], matrix[..., half:])
    return jnp.concatenate([a * cosine - b * sine, b * cosine + a * sine], axis=-1)


def mm(left, right):
    return jnp.dot(left, right, preferred_element_type=F32)


def mm_nt(left, right):
    return lax.dot_general(left, right, (((1,), (1,)), ((), ())), preferred_element_type=F32)


def mm_tn(left, right):
    return lax.dot_general(left, right, (((0,), (0,)), ((), ())), preferred_element_type=F32)


def norm_scale(vector):
    return lax.rsqrt(jnp.mean(vector * vector, axis=-1, keepdims=True) + EPSILON)


def norm_back(upstream, normed, rscale, gain):
    scaled = upstream * gain
    inner = jnp.mean(scaled * normed, axis=-1, keepdims=True)
    return (rscale * (scaled - normed * inner), jnp.sum(upstream * normed, axis=0))


def gather(piece):
    return lax.all_gather(piece, "shard", axis=0, tiled=True)


def scatter(partial):
    return lax.psum_scatter(partial.astype(BF), "shard", scatter_dimension=0, tiled=True).astype(
        F32
    )


def make(n_rep, n_shard):

    def rep_scatter(x):
        if n_rep == 2:
            me = lax.axis_index("rep")
            mine = lax.dynamic_index_in_dim(x, me, 0, keepdims=False)
            other = lax.dynamic_index_in_dim(x, 1 - me, 0, keepdims=False)
            got = lax.ppermute(other.astype(BF), "rep", [(0, 1), (1, 0)])
            return (mine + got.astype(F32)).astype(BF)
        return lax.psum_scatter(x.astype(BF), "rep", scatter_dimension=0, tiled=False)

    def rep_gather(x):
        if n_rep == 2:
            me = lax.axis_index("rep")
            got = lax.ppermute(x, "rep", [(0, 1), (1, 0)])
            first = jnp.where(me == 0, x, got)
            second = jnp.where(me == 0, got, x)
            return jnp.stack([first, second])
        return lax.all_gather(x, "rep", axis=0, tiled=False)

    def rep_sum(x):
        rows = x.shape[0]
        part = rep_scatter(x.reshape(n_rep, rows // n_rep, x.shape[1]))
        return rep_gather(part).reshape(x.shape).astype(F32)

    def grad_back(x, groups):
        rows, cols = x.shape
        own = rows // n_shard
        width = cols // groups
        split = x.reshape(n_shard, n_rep, own // n_rep, cols).transpose(1, 0, 2, 3)
        part = rep_scatter(split)
        part = lax.all_to_all(part, "shard", split_axis=0, concat_axis=0, tiled=True)
        whole = rep_gather(part)
        whole = whole.reshape(n_rep, n_shard, own // n_rep, groups, width)
        return whole.transpose(0, 2, 3, 1, 4).reshape(own, groups * n_shard * width).astype(F32)

    def columns(w, groups):
        rows, cols = w.shape
        w = w.reshape(rows, groups, n_shard, cols // (groups * n_shard))
        w = lax.all_to_all(w, "shard", split_axis=2, concat_axis=0, tiled=True)
        return w.reshape(rows * n_shard, cols // n_shard)

    def shards(
        tokens,
        segment_ids,
        cotangent,
        w_qkv,
        w_out,
        w_gate_up,
        w_down,
        q_gain,
        k_gain,
        attn_gain,
        mlp_gain,
    ):
        count, width = tokens.shape
        heads = H // n_shard
        hw = width // H
        own = width // n_shard
        ff = w_down.shape[0]
        total = count * n_shard
        small = gather(jnp.stack([segment_ids.astype(BF), attn_gain, mlp_gain])[None])
        tokens_g = gather(tokens)
        wq = columns(w_qkv, 3)
        wg = columns(w_gate_up, 2)
        seg = small[:, 0].astype(jnp.int32)
        gain_attn = small[:, 1].reshape(-1).astype(F32)
        gain_mlp = small[:, 2].reshape(-1).astype(F32)
        gain_query = q_gain.astype(F32)
        gain_keys = k_gain.astype(F32)
        cosine, sine = rope_tables(seg, hw)
        cos3 = cosine[:, None, :]
        sin3 = sine[:, None, :]
        qkv = mm(tokens_g, wq)
        query, keys, values_b = (qkv[:, :own], qkv[:, own : 2 * own], qkv[:, 2 * own :].astype(BF))
        squares = jnp.stack([jnp.sum(query * query, axis=-1), jnp.sum(keys * keys, axis=-1)])
        squares = lax.psum(squares, "shard")
        scales = lax.rsqrt(squares / width + EPSILON)
        query_scale, keys_scale = (scales[0][:, None], scales[1][:, None])
        query_hat, keys_hat = (query * query_scale, keys * keys_scale)

        def rot(x, sign):
            return rotate(x.reshape(total, heads, hw), cos3, sign * sin3).reshape(total, own)

        query_rot = rot(query_hat * gain_query, 1.0).astype(BF)
        keys_rot = rot(keys_hat * gain_keys, 1.0).astype(BF)
        slots = jnp.arange(count)
        ok = (seg[:, :, None] == seg[:, None, :]) & (slots[None, :] <= slots[:, None])[None]
        ok = ok[:, None]

        def blocks(x):
            return x.reshape(n_shard, count, heads, hw)

        root = hw ** (-0.5)
        qb, kb, vb = (blocks(query_rot), blocks(keys_rot), blocks(values_b))
        scores = jnp.einsum("bthd,bshd->bhts", qb, kb, preferred_element_type=F32) * root
        scores = jnp.where(ok, scores, -1e30)
        top = jnp.max(scores, axis=-1, keepdims=True)
        lse = top + jnp.log(jnp.sum(jnp.exp(scores - top), axis=-1, keepdims=True))
        probs = jnp.exp(scores - lse)
        probs_b = probs.astype(BF)
        context = jnp.einsum("bhts,bshd->bthd", probs_b, vb, preferred_element_type=F32)
        context_b = context.astype(BF).reshape(total, own)
        attn_raw = scatter(mm(context_b, w_out))
        attn_scale = norm_scale(attn_raw)
        attn_hat = attn_raw * attn_scale
        resid = tokens.astype(F32) + attn_hat * gain_attn
        resid_g = gather(resid.astype(BF))
        gate_up = mm(resid_g, wg)
        gate, up = (gate_up[:, :ff], gate_up[:, ff:])
        sigma = jax.nn.sigmoid(gate)
        activated = gate * sigma
        mixed_b = (activated * up).astype(BF)
        down_raw = scatter(mm(mixed_b, w_down))
        down_scale = norm_scale(down_raw)
        down_hat = down_raw * down_scale
        output = (resid + down_hat * gain_mlp).astype(BF)
        valid = (segment_ids >= 0).astype(F32)[:, None]
        d_out = cotangent.astype(F32) * valid
        d_down, grad_mlp = norm_back(d_out, down_hat, down_scale, gain_mlp)
        d_down_g = gather(d_down.astype(BF))
        d_mixed = mm_nt(d_down_g, w_down)
        d_gate = d_mixed * up * sigma * (1.0 + gate * (1.0 - sigma))
        d_up = d_mixed * activated
        d_gu_b = jnp.concatenate([d_gate, d_up], axis=1).astype(BF)
        d_resid = d_out + scatter(mm_nt(d_gu_b, wg))
        grad_down = rep_sum(mm_tn(mixed_b, d_down_g))
        grad_gu = grad_back(mm_tn(resid_g, d_gu_b), 2)
        d_attn, grad_attn = norm_back(d_resid, attn_hat, attn_scale, gain_attn)
        d_attn_g = gather(d_attn.astype(BF))
        d_context_b = mm_nt(d_attn_g, w_out).astype(BF)
        grad_out = rep_sum(mm_tn(context_b, d_attn_g))
        db = blocks(d_context_b)
        d_values = jnp.einsum("bhts,bthd->bshd", probs_b, db, preferred_element_type=F32)
        d_probs = jnp.einsum("bthd,bshd->bhts", db, vb, preferred_element_type=F32)
        delta = jnp.sum(db.astype(F32) * context, axis=-1).transpose(0, 2, 1)[..., None]
        d_scores_b = (probs * (d_probs - delta) * root).astype(BF)
        d_query_rot = jnp.einsum("bhts,bshd->bthd", d_scores_b, kb, preferred_element_type=F32)
        d_keys_rot = jnp.einsum("bhts,bthd->bshd", d_scores_b, qb, preferred_element_type=F32)
        d_query_norm = rot(d_query_rot, -1.0)
        d_keys_norm = rot(d_keys_rot, -1.0)
        grad_query = jnp.sum(d_query_norm * query_hat, axis=0)
        grad_keys = jnp.sum(d_keys_norm * keys_hat, axis=0)
        query_up = d_query_norm * gain_query
        keys_up = d_keys_norm * gain_keys
        inner = jnp.stack(
            [jnp.sum(query_up * query_hat, axis=-1), jnp.sum(keys_up * keys_hat, axis=-1)]
        )
        inner = lax.psum(inner, "shard") / width
        d_query = query_scale * (query_up - query_hat * inner[0][:, None])
        d_keys = keys_scale * (keys_up - keys_hat * inner[1][:, None])
        d_qkv_b = jnp.concatenate([d_query, d_keys, d_values.reshape(total, own)], axis=1).astype(
            BF
        )
        grad_tokens = d_resid + scatter(mm_nt(d_qkv_b, wq))
        grad_qkv = grad_back(mm_tn(tokens_g, d_qkv_b), 3)
        gains_local = lax.psum_scatter(
            jnp.stack([grad_attn, grad_mlp]), "shard", scatter_dimension=1, tiled=True
        )
        gains = lax.psum(jnp.concatenate([gains_local, jnp.stack([grad_query, grad_keys])]), "rep")
        return (
            output,
            grad_tokens,
            grad_qkv,
            grad_out,
            grad_gu,
            grad_down,
            gains[2],
            gains[3],
            gains[0],
            gains[1],
        )

    return shards


def solution(mesh):
    rows = P(("rep", "shard"), None)
    return jax.shard_map(
        make(mesh.shape["rep"], mesh.shape["shard"]),
        mesh=mesh,
        in_specs=(rows, P(("rep", "shard")), rows) + (P("shard", None),) * 4 + (P("shard"),) * 4,
        out_specs=(rows, rows) + (P("shard", None),) * 4 + (P("shard"),) * 4,
        check_vma=False,
    )
```

profile of v0, /device:TPU:0, one launch (start us, length us, event | category | flops | bytes accessed | tf_op | source)
XLA Modules:
  0.0 1212.3 jit_solution(16660373175642401086)
XLA Ops:
  13.3 7.5 all-to-all-start
  20.9 58.7 %all-gather.1 = bf16[16,3,128]{2,1,0:T(4,128)(2,1)S(1)} all-gather(bf16[1,3,128]{2,1,0:T(4,128)(2,1)S(1)} %maximum_bitcast_fusion.2), channel_id=2, replica_groups=mesh['rep'=2,'shard'=16] {'shard'}, dimensions={0}, use_global_device_ids=true | all-gather | bytes 13056 | tf_op jit(solution)/shard_map/all_gather | solution.py:59
  83.7 29.8 %all-gather.7.cloned.1.call-done = bf16[2048,2048]{1,0:T(8,128)(2,1)} async-done(((bf16[128,2048]{1,0:T(8,128)(2,1)}), bf16[2048,2048]{1,0:T(8,128)(2,1)}) %all-gather.7.cloned.1.call-update) | async-done | bytes 8388624 | tf_op jit(solution)/shard_map/all_gather | solution.py:59
  122.4 58.7 %psum.21 = f32[2,2048]{1,0:T(2,128)S(1)} all-reduce(f32[2,2048]{1,0:T(2,128)S(1)} %pad_maximum_fusion.10), channel_id=1, replica_groups=mesh['rep'=2,'shard'=16] {'shard'}, use_global_device_ids=true, to_apply=%region_2.3 | all-reduce | flops 4096 | bytes 32768 | tf_op jit(solution)/shard_map/psum | solution.py:144
  201.9 100.9 %reduce-scatter.8.cloned.1.call-done = bf16[128,2048]{1,0:T(8,128)(2,1)} async-done(((bf16[2048,2048]{1,0:T(8,128)(2,1)}), bf16[128,2048]{1,0:T(8,128)(2,1)}) %reduce-scatter.8.cloned.1.call-update) | async-done | bytes 524304 | tf_op jit(solution)/shard_map/reduce_scatter | solution.py:63
  315.5 142.0 %all_to_all.40 = bf16[128,2,16,512]{0,3,1,2:T(8,128)(2,1)S(1)} all-to-all(bf16[128,2,16,512]{0,3,1,2:T(8,128)(2,1)S(1)} %copy.121), channel_id=1, replica_groups=mesh['rep'=2,'shard'=16] {'shard'}, dimensions={2} | all-to-all | bytes 8388608 | tf_op jit(solution)/shard_map/all_to_all | solution.py:107
  462.2 12.6 %fusion.3 = f32[2048,1024]{0,1:T(8,128)S(1)} fusion(bf16[2048,2048]{1,0:T(8,128)(2,1)} %all-gather.9.cloned.1.call-done, bf16[128,8,16,128]{3,2,1,0:T(8,128)(2,1)} %bitcast.203), kind=kOutput, calls=%fused_computation.8 | convolution fusion | flops 8589934592 | bytes 20971520 | tf_op jit(solution)/shard_map/dot_general | solution.py:37
  486.3 103.5 %reduce-scatter.10.cloned.1.call-done = bf16[128,2048]{1,0:T(8,128)(2,1)} async-done(((bf16[2048,2048]{1,0:T(8,128)(2,1)}), bf16[128,2048]{1,0:T(8,128)(2,1)}) %reduce-scatter.10.cloned.1.call-update) | async-done | bytes 524304 | tf_op jit(solution)/shard_map/reduce_scatter | solution.py:63
  595.4 73.9 %all-gather.11.cloned.1.call-done = bf16[2048,2048]{1,0:T(8,128)(2,1)} async-done(((bf16[128,2048]{1,0:T(8,128)(2,1)}), bf16[2048,2048]{1,0:T(8,128)(2,1)}) %all-gather.11.cloned.1.call-update) | async-done | bytes 8388624 | tf_op jit(solution)/shard_map/all_gather | solution.py:59
  669.3 10.6 multiply_convert_fusion.1
  681.9 11.8 convolution_convert_fusion.1
  693.8 102.1 %reduce-scatter.12.cloned.1.call-done = bf16[128,2048]{1,0:T(8,128)(2,1)} async-done(((bf16[2048,2048]{1,0:T(8,128)(2,1)}), bf16[128,2048]{1,0:T(8,128)(2,1)}) %reduce-scatter.12.cloned.1.call-update) | async-done | bytes 524304 | tf_op jit(solution)/shard_map/reduce_scatter | solution.py:63
  800.5 12.6 %fusion.9 = f32[2048,1024]{1,0:T(8,128)S(1)} fusion(bf16[2048,2048]{1,0:T(8,128)(2,1)} %all-gather.9.cloned.1.call-done, bf16[2048,512]{0,1:T(8,128)(2,1)} %copy-done.35, bf16[2048,512]{0,1:T(8,128)(2,1)} %copy-done.34), kind=kOutput, calls=%fused_computation.23 | convolution fusion | flops 8598323200 | bytes 20971520 | tf_op jit(solution)/shard_map/dot_general | solution.py:45
  821.1 53.2 %all-gather.13.cloned.1.call-done = bf16[2048,2048]{1,0:T(8,128)(2,1)} async-done(((bf16[128,2048]{1,0:T(8,128)(2,1)}), bf16[2048,2048]{1,0:T(8,128)(2,1)}) %all-gather.13.cloned.1.call-update) | async-done | bytes 8388624 | tf_op jit(solution)/shard_map/all_gather | solution.py:59
  899.3 60.0 %psum.22 = f32[2,2048]{1,0:T(2,128)S(1)} all-reduce(f32[2,2048]{1,0:T(2,128)S(1)} %pad_maximum_fusion.11), channel_id=1, replica_groups=mesh['rep'=2,'shard'=16] {'shard'}, use_global_device_ids=true, to_apply=%region_16.17 | all-reduce | flops 4096 | bytes 32768 | tf_op jit(solution)/shard_map/psum | solution.py:216
  963.0 9.8 convolution_convert_fusion
  991.7 24.1 %collective-permute-done.6 = bf16[256,2048]{1,0:T(8,128)(2,1)S(1)} collective-permute-done((bf16[256,2048]{1,0:T(8,128)(2,1)S(1)}, bf16[256,2048]{1,0:T(8,128)(2,1)S(1)}, u32[]{:S(2)}, u32[]{:S(2)}) %collective-permute-start.6) | collective-permute-done | bytes 1048608 | tf_op jit(solution)/shard_map/ppermute | solution.py:75
  1018.5 20.4 %all-to-all-done.3 = bf16[16,64,1024]{2,1,0:T(8,128)(2,1)} async-done(((bf16[16,64,1024]{2,1,0:T(8,128)(2,1)}), bf16[16,64,1024]{2,1,0:T(8,128)(2,1)}, u32[]{:S(2)}, u32[]{:S(2)}) %all-to-all-start.3) | async-done | bytes 2097184 | tf_op jit(solution)/shard_map/all_to_all | solution.py:99
  1043.8 8.6 convolution_bitcast_fusion
  1061.4 22.4 %collective-permute-done.5 = bf16[16,64,1024]{2,1,0:T(8,128)(2,1)} collective-permute-done((bf16[16,64,1024]{2,1,0:T(8,128)(2,1)}, bf16[16,64,1024]{2,1,0:T(8,128)(2,1)}, u32[]{:S(2)}, u32[]{:S(2)}) %collective-permute-start.5) | collective-permute-done | bytes 2097184 | tf_op jit(solution)/shard_map/ppermute | solution.py:82
  1110.0 32.8 %all-to-all-start.2 = ((bf16[16,64,384]{2,1,0:T(8,128)(2,1)}), bf16[16,64,384]{2,1,0:T(8,128)(2,1)}, u32[]{:S(2)}, u32[]{:S(2)}) async-start(bf16[16,64,384]{2,1,0:T(8,128)(2,1)} %fusion.15), calls=%async_computation.6 | async-start | bytes 1572864 | tf_op jit(solution)/shard_map/all_to_all | solution.py:99
  1153.1 9.4 reshape.428
  1165.2 7.6 psum.23
  1175.3 16.9 %collective-permute-done.1 = bf16[16,64,384]{2,1,0:T(8,128)(2,1)S(1)} collective-permute-done((bf16[16,64,384]{2,1,0:T(8,128)(2,1)}, bf16[16,64,384]{2,1,0:T(8,128)(2,1)S(1)}, u32[]{:S(2)}, u32[]{:S(2)}) %collective-permute-start.1) | collective-permute-done | bytes 786464 | tf_op jit(solution)/shard_map/ppermute | solution.py:82
  (212 shorter events, 207.6 us)
Async XLA Ops:
  7.2 472.2 %copy-start = (bf16[512,2048]{1,0:T(8,128)(2,1)S(1)}, bf16[512,2048]{1,0:T(8,128)(2,1)}, u32[]{:S(2)}) copy-start(bf16[512,2048]{1,0:T(8,128)(2,1)} %param.17) | copy-start | bytes 6291460
  7.2 106.3 %all-gather.7.cloned.1.call-start = ((), (), s32[]{:S(2)}) async-start(), calls=%async_computation.9 | async-start | bytes 8912896 | tf_op jit(solution)/shard_map/all_gather | solution.py:59
  13.3 66.8 %all-to-all-start = ((bf16[128,3,16,128]{0,3,1,2:T(8,128)(2,1)}), bf16[128,3,16,128]{0,3,1,2:T(8,128)(2,1)}, u32[]{:S(2)}, u32[]{:S(2)}) async-start(bf16[128,3,16,128]{0,3,1,2:T(8,128)(2,1)} %copy.114), calls=%async_computation | async-start | bytes 3145728 | tf_op jit(solution)/shard_map/all_to_all | solution.py:107
  20.8 282.0 %reduce-scatter.8.cloned.1.call-start = ((), (), s32[]{:S(2)}) async-start(), calls=%async_computation.10 | async-start | bytes 8912896 | tf_op jit(solution)/shard_map/reduce_scatter | solution.py:63
  201.8 260.3 %all-gather.9.cloned.1.call-start = ((), (), s32[]{:S(2)}) async-start(), calls=%async_computation.11 | async-start | bytes 8912896 | tf_op jit(solution)/shard_map/all_gather | solution.py:59
  306.3 283.5 %reduce-scatter.10.cloned.1.call-start = ((), (), s32[]{:S(2)}) async-start(), calls=%async_computation.12 | async-start | bytes 8912896 | tf_op jit(solution)/shard_map/reduce_scatter | solution.py:63
  486.3 183.0 %all-gather.11.cloned.1.call-start = ((), (), s32[]{:S(2)}) async-start(), calls=%async_computation.13 | async-start | bytes 8912896 | tf_op jit(solution)/shard_map/all_gather | solution.py:59
  595.2 200.7 %reduce-scatter.12.cloned.1.call-start = ((), (), s32[]{:S(2)}) async-start(), calls=%async_computation.14 | async-start | bytes 8912896 | tf_op jit(solution)/shard_map/reduce_scatter | solution.py:63
  693.7 102.2 %copy-start.6 = (bf16[128,2048]{1,0:T(8,128)(2,1)S(1)}, bf16[128,2048]{1,0:T(8,128)(2,1)}, u32[]{:S(2)}) copy-start(bf16[128,2048]{1,0:T(8,128)(2,1)} %reduce-scatter.8.cloned.1.call-done) | copy-start | bytes 1572868
  693.7 103.8 %copy-start.7 = (bf16[128,2048]{1,0:T(8,128)(2,1)S(1)}, bf16[128,2048]{1,0:T(8,128)(2,1)}, u32[]{:S(2)}) copy-start(bf16[128,2048]{1,0:T(8,128)(2,1)} %reduce-scatter.10.cloned.1.call-done) | copy-start | bytes 1572868
  693.7 103.8 %copy-start.12 = (bf16[128,2048]{1,0:T(8,128)(2,1)S(1)}, bf16[128,2048]{1,0:T(8,128)(2,1)}, u32[]{:S(2)}) copy-start(bf16[128,2048]{1,0:T(8,128)(2,1)} %param.11) | copy-start | bytes 1572868
  693.7 180.6 %all-gather.13.cloned.1.call-start = ((), (), s32[]{:S(2)}) async-start(), calls=%async_computation.15 | async-start | bytes 8912896 | tf_op jit(solution)/shard_map/all_gather | solution.py:59
  800.2 362.2 %reduce-scatter.16.cloned.1.call-start = ((), (), s32[]{:S(2)}) async-start(), calls=%async_computation.17 | async-start | bytes 1114112
  818.1 154.7 %collective-permute-start.4 = (bf16[16,64,1024]{2,1,0:T(8,128)(2,1)}, bf16[16,64,1024]{2,1,0:T(8,128)(2,1)}, u32[]{:S(2)}, u32[]{:S(2)}) collective-permute-start(bf16[16,64,1024]{2,1,0:T(8,128)(2,1)} %fusion.10), channel_id=1, source_target_pairs={{0,16},{16,0},{1,17},{17,1},{2,18},{18,2},{3,19},{19,3},{4,20},{20... | collective-permute-start | bytes 6291464 | tf_op jit(solution)/shard_map/ppermute | solution.py:75
  821.1 382.1 %reduce-scatter.14.cloned.1.call-start = ((), (), s32[]{:S(2)}) async-start(), calls=%async_computation.16 | async-start | bytes 8912896 | tf_op jit(solution)/shard_map/reduce_scatter | solution.py:63
  977.8 61.1 %all-to-all-start.3 = ((bf16[16,64,1024]{2,1,0:T(8,128)(2,1)}), bf16[16,64,1024]{2,1,0:T(8,128)(2,1)}, u32[]{:S(2)}, u32[]{:S(2)}) async-start(bf16[16,64,1024]{2,1,0:T(8,128)(2,1)} %fusion.5), calls=%async_computation.7 | async-start | bytes 4194304 | tf_op jit(solution)/shard_map/all_to_all | solution.py:99
  990.2 25.5 %collective-permute-start.6 = (bf16[256,2048]{1,0:T(8,128)(2,1)S(1)}, bf16[256,2048]{1,0:T(8,128)(2,1)S(1)}, u32[]{:S(2)}, u32[]{:S(2)}) collective-permute-start(bf16[256,2048]{1,0:T(8,128)(2,1)S(1)} %fusion.45), channel_id=1, source_target_pairs={{0,16},{16,0},{1,17},{17,1},{2,18},{18,2},{3,19},{19,3},{4,20},{20... | collective-permute-start | bytes 3145736 | tf_op jit(solution)/shard_map/ppermute | solution.py:75
  1016.0 24.9 %collective-permute-start.7 = (bf16[256,2048]{1,0:T(8,128)(2,1)S(1)}, bf16[256,2048]{1,0:T(8,128)(2,1)}, u32[]{:S(2)}, u32[]{:S(2)}) collective-permute-start(bf16[256,2048]{1,0:T(8,128)(2,1)S(1)} %fusion.11), channel_id=1, source_target_pairs={{0,16},{16,0},{1,17},{17,1},{2,18},{18,2},{3,19},{19,3},{4,20},{20... | collective-permute-start | bytes 3145736 | tf_op jit(solution)/shard_map/ppermute | solution.py:82
  1039.0 44.9 %collective-permute-start.5 = (bf16[16,64,1024]{2,1,0:T(8,128)(2,1)}, bf16[16,64,1024]{2,1,0:T(8,128)(2,1)}, u32[]{:S(2)}, u32[]{:S(2)}) collective-permute-start(bf16[16,64,1024]{2,1,0:T(8,128)(2,1)} %all-to-all-done.3), channel_id=1, source_target_pairs={{0,16},{16,0},{1,17},{17,1},{2,18},{18,2},{3,19},{19,3},{4,20},{20... | collective-permute-start | bytes 6291464 | tf_op jit(solution)/shard_map/ppermute | solution.py:82
  1055.8 52.1 %collective-permute-start = (bf16[16,64,384]{2,1,0:T(8,128)(2,1)}, bf16[16,64,384]{2,1,0:T(8,128)(2,1)}, u32[]{:S(2)}, u32[]{:S(2)}) collective-permute-start(bf16[16,64,384]{2,1,0:T(8,128)(2,1)} %fusion.50), channel_id=1, source_target_pairs={{0,16},{16,0},{1,17},{17,1},{2,18},{18,2},{3,19},{19,3},{4,20},{20... | collective-permute-start | bytes 2359304 | tf_op jit(solution)/shard_map/ppermute | solution.py:75
  1110.0 63.3 %all-to-all-start.2 = ((bf16[16,64,384]{2,1,0:T(8,128)(2,1)}), bf16[16,64,384]{2,1,0:T(8,128)(2,1)}, u32[]{:S(2)}, u32[]{:S(2)}) async-start(bf16[16,64,384]{2,1,0:T(8,128)(2,1)} %fusion.15), calls=%async_computation.6 | async-start | bytes 1572864 | tf_op jit(solution)/shard_map/all_to_all | solution.py:99
  1147.9 15.4 %collective-permute-start.2 = (bf16[64,2048]{1,0:T(8,128)(2,1)S(1)}, bf16[64,2048]{1,0:T(8,128)(2,1)}, u32[]{:S(2)}, u32[]{:S(2)}) collective-permute-start(bf16[64,2048]{1,0:T(8,128)(2,1)S(1)} %fusion.81), channel_id=1, source_target_pairs={{0,16},{16,0},{1,17},{17,1},{2,18},{18,2},{3,19},{19,3},{4,20},{20... | collective-permute-start | bytes 786440 | tf_op jit(solution)/shard_map/ppermute | solution.py:75
  1164.4 9.7 collective-permute-start.3
  1173.3 18.9 %collective-permute-start.1 = (bf16[16,64,384]{2,1,0:T(8,128)(2,1)}, bf16[16,64,384]{2,1,0:T(8,128)(2,1)S(1)}, u32[]{:S(2)}, u32[]{:S(2)}) collective-permute-start(bf16[16,64,384]{2,1,0:T(8,128)(2,1)} %all-to-all-done.2), channel_id=1, source_target_pairs={{0,16},{16,0},{1,17},{17,1},{2,18},{18,2},{3,19},{19,3},{4,20},{20... | collective-permute-start | bytes 2359304 | tf_op jit(solution)/shard_map/ppermute | solution.py:82
  (32 other events, 510.7 us)
Sparse Core Ops, SparseCore 0:
  10.2 103.3 all-gather.6
  202.0 100.8 reduce-scatter.7
  306.4 134.0 all-gather.8
  486.4 103.4 reduce-scatter.9
  595.3 73.9 all-gather.10
  693.8 102.0 reduce-scatter.11
  800.3 73.9 all-gather.12
  877.9 56.2 reduce-scatter.15
  972.9 130.3 reduce-scatter.13
where the time goes:
time: 1220 us; the launch traced here: 1210 us
  waiting for transfers between devices  549 us (45%)
  blocking collectives  327 us (27%)
  matrix products  110 us (9%)
  local copies, waits for them, and re-layouts  96.8 us (8%)
  other arithmetic  59.2 us (5%)
  starting transfers between devices  56 us (5%)
  between operations  14.8 us (1%)
    reduce_scatter x4, waiting for transfers between devices, scatter(): lax.psum_scatter(partial.astype(BF), 'shard', scatter_dimension=0, tiled=...  307 us
    all_gather x4, waiting for transfers between devices, gather(): return lax.all_gather(piece, 'shard', axis=0, tiled=True)  157 us
    all_to_all x1, blocking collectives, columns(): w = lax.all_to_all(w, 'shard', split_axis=2, concat_axis=0, tiled=True)  142 us
    psum x1, blocking collectives, shards(): inner = lax.psum(inner, 'shard') / width  60 us
    psum x1, blocking collectives, shards(): squares = lax.psum(squares, 'shard')  58.7 us
    all_gather x1, blocking collectives, gather(): return lax.all_gather(piece, 'shard', axis=0, tiled=True)  58.7 us
    ppermute x4, waiting for transfers between devices, rep_gather(): got = lax.ppermute(x, 'rep', [(0, 1), (1, 0)])  40 us
    dot_general x4, matrix products, mm_nt(): lax.dot_general(left, right, (((1,), (1,)), ((), ())), preferred_element_...  37.9 us
  transfers between devices with their start and end apart: 20, of which 11 were waited for; matrix products, arithmetic and copies ran while one was open for 14% of the time, Pallas kernels for 0%

commit v1 on v0

--- a/solution.py
+++ b/solution.py
@@ -56,7 +56,9 @@
 
 
 def gather(piece):
-    return lax.all_gather(piece, "shard", axis=0, tiled=True)
+    return jnp.concatenate(
+        lax.all_to_all(jnp.stack([piece] * lax.axis_size("shard")), "shard", 0, 0), axis=0
+    )
 
 
 def scatter(partial):

time: 1220 us -> 1730 us (1.42)
  waiting for transfers between devices: 549 us -> 886 us
  blocking collectives: 327 us -> 421 us
  local copies, waits for them, and re-layouts: 96.8 us -> 150 us
  starting transfers between devices: 56 us -> 75.5 us
    all_to_all x0 -> x4, waiting for transfers between devices: none -> 415 us  [gather(): lax.all_to_all(jnp.stack([piece] * lax.axis_size('shard')), 'shard', 0, 0)]
    all_to_all x0 -> x1, blocking collectives: none -> 186 us  [gather(): lax.all_to_all(jnp.stack([piece] * lax.axis_size('shard')), 'shard', 0, 0)]
    all_gather x4 -> x0, waiting for transfers between devices: 157 us -> none  [gather(): return lax.all_gather(piece, 'shard', axis=0, tiled=True)]
    all_to_all x1, blocking collectives: 142 us -> 40.9 us  [columns(): w = lax.all_to_all(w, 'shard', split_axis=2, concat_axis=0, tiled=True)]
    reduce_scatter x4, waiting for transfers between devices: 307 us -> 385 us  [scatter(): lax.psum_scatter(partial.astype(BF), 'shard', scatter_dimension=0, tiled=...]
    all_gather x1 -> x0, blocking collectives: 58.7 us -> none  [gather(): return lax.all_gather(piece, 'shard', axis=0, tiled=True)]
    psum x1, blocking collectives: 58.7 us -> 92.7 us  [shards(): squares = lax.psum(squares, 'shard')]
    psum x1, blocking collectives: 60 us -> 92.8 us  [shards(): inner = lax.psum(inner, 'shard') / width]
  transfers between devices with their start and end apart: 20 -> 20, of which waited for: 11 -> 12; matrix products, arithmetic and copies ran while one was open for 14% -> 11% of each run, Pallas kernels for 0% -> 0%
where the time goes in v1:
time: 1730 us; the launch traced here: 1720 us
  waiting for transfers between devices  886 us (51%)
  blocking collectives  421 us (24%)
  local copies, waits for them, and re-layouts  150 us (9%)
  matrix products  108 us (6%)
  starting transfers between devices  75.5 us (4%)
  other arithmetic  61.7 us (4%)
    all_to_all x4, waiting for transfers between devices, gather(): lax.all_to_all(jnp.stack([piece] * lax.axis_size('shard')), 'shard', 0, 0)  415 us
    reduce_scatter x4, waiting for transfers between devices, scatter(): lax.psum_scatter(partial.astype(BF), 'shard', scatter_dimension=0, tiled=...  385 us
    all_to_all x1, blocking collectives, gather(): lax.all_to_all(jnp.stack([piece] * lax.axis_size('shard')), 'shard', 0, 0)  186 us
    psum x1, blocking collectives, shards(): inner = lax.psum(inner, 'shard') / width  92.8 us
    psum x1, blocking collectives, shards(): squares = lax.psum(squares, 'shard')  92.7 us
    ppermute x4, waiting for transfers between devices, rep_gather(): got = lax.ppermute(x, 'rep', [(0, 1), (1, 0)])  41.9 us
    all_to_all x1, blocking collectives, columns(): w = lax.all_to_all(w, 'shard', split_axis=2, concat_axis=0, tiled=True)  40.9 us
    all_to_all x2, starting transfers between devices, grad_back(): lax.all_to_all(part, 'shard', split_axis=0, concat_axis=0, tiled=True)  37.5 us
  transfers between devices with their start and end apart: 20, of which 12 were waited for; matrix products, arithmetic and copies ran while one was open for 11% of the time, Pallas kernels for 0%

profile of v1, /device:TPU:0, one launch (start us, length us, event | category | flops | bytes accessed | tf_op | source)
XLA Modules:
  0.0 1717.4 jit_solution(5755267799322481953)
XLA Ops:
  23.2 40.9 %all_to_all.65 = bf16[128,3,16,128]{0,3,1,2:T(8,128)(2,1)} all-to-all(bf16[128,3,16,128]{0,3,1,2:T(8,128)(2,1)} %copy.119), channel_id=1, replica_groups=mesh['rep'=2,'shard'=16] {'shard'}, dimensions={2} | all-to-all | bytes 3145728 | tf_op jit(solution)/shard_map/all_to_all | solution.py:109
  78.1 146.4 %all-to-all-done = bf16[16,128,2048]{2,1,0:T(8,128)(2,1)} async-done(((bf16[16,128,2048]{2,1,0:T(8,128)(2,1)}), bf16[16,128,2048]{2,1,0:T(8,128)(2,1)}, u32[]{:S(2)}, u32[]{:S(2)}) %all-to-all-start) | async-done | bytes 8388640 | tf_op jit(solution)/shard_map/all_to_all | solution.py:60
  233.4 92.7 %psum.21 = f32[2,2048]{1,0:T(2,128)S(1)} all-reduce(f32[2,2048]{1,0:T(2,128)S(1)} %pad_maximum_fusion.10), channel_id=1, replica_groups=mesh['rep'=2,'shard'=16] {'shard'}, use_global_device_ids=true, to_apply=%region_2.3 | all-reduce | flops 4096 | bytes 32768 | tf_op jit(solution)/shard_map/psum | solution.py:146
  363.2 145.7 %reduce-scatter.8.cloned.1.call-done = bf16[128,2048]{1,0:T(8,128)(2,1)} async-done(((bf16[2048,2048]{1,0:T(8,128)(2,1)}), bf16[128,2048]{1,0:T(8,128)(2,1)}) %reduce-scatter.8.cloned.1.call-update) | async-done | bytes 524304 | tf_op jit(solution)/shard_map/reduce_scatter | solution.py:65
  532.2 143.6 %all-to-all-done.3 = bf16[16,128,2048]{1,2,0:T(8,128)(2,1)} async-done(((bf16[16,128,2048]{1,2,0:T(8,128)(2,1)}), bf16[16,128,2048]{1,2,0:T(8,128)(2,1)}, u32[]{:S(2)}, u32[]{:S(2)}) %all-to-all-start.3) | async-done | bytes 8388640 | tf_op jit(solution)/shard_map/all_to_all | solution.py:60
  675.7 12.2 copy.126
  688.0 12.5 fusion.1
  712.7 134.8 %reduce-scatter.10.cloned.1.call-done = bf16[128,2048]{1,0:T(8,128)(2,1)} async-done(((bf16[2048,2048]{1,0:T(8,128)(2,1)}), bf16[128,2048]{1,0:T(8,128)(2,1)}) %reduce-scatter.10.cloned.1.call-update) | async-done | bytes 524304 | tf_op jit(solution)/shard_map/reduce_scatter | solution.py:65
  853.0 186.5 %all_to_all.66 = bf16[16,128,2048]{2,1,0:T(8,128)(2,1)} all-to-all(bf16[16,128,2048]{2,1,0:T(8,128)(2,1)S(1)} %stack.74), channel_id=1, replica_groups=mesh['rep'=2,'shard'=16] {'shard'}, dimensions={0} | all-to-all | bytes 16777216 | tf_op jit(solution)/shard_map/all_to_all | solution.py:60
  1039.5 9.6 multiply_convert_fusion.1
  1051.2 11.8 convolution_convert_fusion.1
  1063.0 104.7 %reduce-scatter.12.cloned.1.call-done = bf16[128,2048]{1,0:T(8,128)(2,1)} async-done(((bf16[2048,2048]{1,0:T(8,128)(2,1)}), bf16[128,2048]{1,0:T(8,128)(2,1)}) %reduce-scatter.12.cloned.1.call-update) | async-done | bytes 524304 | tf_op jit(solution)/shard_map/reduce_scatter | solution.py:65
  1181.4 12.5 copy.141
  1193.9 12.0 fusion.4
  1213.8 124.0 %all-to-all-done.6 = bf16[16,128,2048]{2,1,0:T(8,128)(2,1)} async-done(((bf16[16,128,2048]{2,1,0:T(8,128)(2,1)}), bf16[16,128,2048]{2,1,0:T(8,128)(2,1)}, u32[]{:S(2)}, u32[]{:S(2)}) %all-to-all-start.6) | async-done | bytes 8388640 | tf_op jit(solution)/shard_map/all_to_all | solution.py:60
  1363.8 92.8 %psum.22 = f32[2,2048]{1,0:T(2,128)S(1)} all-reduce(f32[2,2048]{1,0:T(2,128)S(1)} %pad_maximum_fusion.11), channel_id=1, replica_groups=mesh['rep'=2,'shard'=16] {'shard'}, use_global_device_ids=true, to_apply=%region_16.17 | all-reduce | flops 4096 | bytes 32768 | tf_op jit(solution)/shard_map/psum | solution.py:218
  1489.2 23.9 %collective-permute-done.6 = bf16[256,2048]{1,0:T(8,128)(2,1)S(1)} collective-permute-done((bf16[256,2048]{1,0:T(8,128)(2,1)S(1)}, bf16[256,2048]{1,0:T(8,128)(2,1)S(1)}, u32[]{:S(2)}, u32[]{:S(2)}) %collective-permute-start.6) | collective-permute-done | bytes 1048608 | tf_op jit(solution)/shard_map/ppermute | solution.py:77
  1515.9 20.5 %all-to-all-done.8 = bf16[16,64,1024]{2,1,0:T(8,128)(2,1)} async-done(((bf16[16,64,1024]{2,1,0:T(8,128)(2,1)}), bf16[16,64,1024]{2,1,0:T(8,128)(2,1)}, u32[]{:S(2)}, u32[]{:S(2)}) %all-to-all-start.8) | async-done | bytes 2097184 | tf_op jit(solution)/shard_map/all_to_all | solution.py:101
  1557.0 24.3 %collective-permute-done.5 = bf16[16,64,1024]{2,1,0:T(8,128)(2,1)} collective-permute-done((bf16[16,64,1024]{2,1,0:T(8,128)(2,1)}, bf16[16,64,1024]{2,1,0:T(8,128)(2,1)}, u32[]{:S(2)}, u32[]{:S(2)}) %collective-permute-start.5) | collective-permute-done | bytes 2097184 | tf_op jit(solution)/shard_map/ppermute | solution.py:84
  1602.4 32.8 %all-to-all-start.7 = ((bf16[16,64,384]{2,1,0:T(8,128)(2,1)}), bf16[16,64,384]{2,1,0:T(8,128)(2,1)}, u32[]{:S(2)}, u32[]{:S(2)}) async-start(bf16[16,64,384]{2,1,0:T(8,128)(2,1)} %fusion.14), calls=%async_computation.11 | async-start | bytes 1572864 | tf_op jit(solution)/shard_map/all_to_all | solution.py:101
  1635.2 10.4 convert_bitcast_fusion
  1645.6 11.5 copy.143
  1657.1 9.4 reshape.454
  1679.8 17.3 %collective-permute-done.1 = bf16[16,64,384]{2,1,0:T(8,128)(2,1)S(1)} collective-permute-done((bf16[16,64,384]{2,1,0:T(8,128)(2,1)}, bf16[16,64,384]{2,1,0:T(8,128)(2,1)S(1)}, u32[]{:S(2)}, u32[]{:S(2)}) %collective-permute-start.1) | collective-permute-done | bytes 786464 | tf_op jit(solution)/shard_map/ppermute | solution.py:84
  (246 shorter events, 269.8 us)
Async XLA Ops:
  7.2 698.0 %copy-start = (bf16[512,2048]{1,0:T(8,128)(2,1)S(1)}, bf16[512,2048]{1,0:T(8,128)(2,1)}, u32[]{:S(2)}) copy-start(bf16[512,2048]{1,0:T(8,128)(2,1)} %param.17) | copy-start | bytes 6291460
  9.3 13.9 all-to-all-start.2
  68.6 155.8 %all-to-all-start = ((bf16[16,128,2048]{2,1,0:T(8,128)(2,1)}), bf16[16,128,2048]{2,1,0:T(8,128)(2,1)}, u32[]{:S(2)}, u32[]{:S(2)}) async-start(bf16[16,128,2048]{2,1,0:T(8,128)(2,1)} %stack.64), calls=%async_computation | async-start | bytes 16777216 | tf_op jit(solution)/shard_map/all_to_all | solution.py:60
  73.9 434.9 %reduce-scatter.8.cloned.1.call-start = ((), (), s32[]{:S(2)}) async-start(), calls=%async_computation.14 | async-start | bytes 8912896 | tf_op jit(solution)/shard_map/reduce_scatter | solution.py:65
  74.0 252.2 %copy-start.37 = (f32[128]{0:T(128)}, f32[128]{0:T(128)S(1)}, u32[]{:S(2)}) copy-start(f32[128]{0:T(128)S(1)} %convert_element_type.225) | copy-start | bytes 1540
  74.0 254.0 %copy-start.41 = (f32[64]{0:T(128)}, f32[64]{0:T(128)S(1)}, u32[]{:S(2)}) copy-start(f32[64]{0:T(128)S(1)} %multiply_power_fusion) | copy-start | bytes 772
  74.5 253.5 %copy-start.35 = (f32[2048]{0:T(1024)}, f32[2048]{0:T(1024)S(1)}, u32[]{:S(2)}) copy-start(f32[2048]{0:T(1024)S(1)} %convert_bitcast_fusion.2) | copy-start | bytes 24580
  358.4 155.9 %all-to-all-start.4 = ((bf16[128,2,16,512]{0,3,1,2:T(8,128)(2,1)}), bf16[128,2,16,512]{0,3,1,2:T(8,128)(2,1)}, u32[]{:S(2)}, u32[]{:S(2)}) async-start(bf16[128,2,16,512]{0,3,1,2:T(8,128)(2,1)} %copy.128), calls=%async_computation.5 | async-start | bytes 8388608 | tf_op jit(solution)/shard_map/all_to_all | solution.py:109
  520.4 155.3 %all-to-all-start.3 = ((bf16[16,128,2048]{1,2,0:T(8,128)(2,1)}), bf16[16,128,2048]{1,2,0:T(8,128)(2,1)}, u32[]{:S(2)}, u32[]{:S(2)}) async-start(bf16[16,128,2048]{1,2,0:T(8,128)(2,1)} %stack.73), calls=%async_computation.4 | async-start | bytes 16777216 | tf_op jit(solution)/shard_map/all_to_all | solution.py:60
  525.2 322.3 %reduce-scatter.10.cloned.1.call-start = ((), (), s32[]{:S(2)}) async-start(), calls=%async_computation.15 | async-start | bytes 8912896 | tf_op jit(solution)/shard_map/reduce_scatter | solution.py:65
  712.1 455.6 %reduce-scatter.12.cloned.1.call-start = ((), (), s32[]{:S(2)}) async-start(), calls=%async_computation.16 | async-start | bytes 8912896 | tf_op jit(solution)/shard_map/reduce_scatter | solution.py:65
  1176.1 161.7 %all-to-all-start.6 = ((bf16[16,128,2048]{2,1,0:T(8,128)(2,1)}), bf16[16,128,2048]{2,1,0:T(8,128)(2,1)}, u32[]{:S(2)}, u32[]{:S(2)}) async-start(bf16[16,128,2048]{2,1,0:T(8,128)(2,1)} %stack.75), calls=%async_computation.9 | async-start | bytes 16777216 | tf_op jit(solution)/shard_map/all_to_all | solution.py:60
  1180.9 485.6 %reduce-scatter.16.cloned.1.call-start = ((), (), s32[]{:S(2)}) async-start(), calls=%async_computation.18 | async-start | bytes 1114112
  1210.9 259.6 %collective-permute-start.4 = (bf16[16,64,1024]{2,1,0:T(8,128)(2,1)}, bf16[16,64,1024]{2,1,0:T(8,128)(2,1)}, u32[]{:S(2)}, u32[]{:S(2)}) collective-permute-start(bf16[16,64,1024]{2,1,0:T(8,128)(2,1)} %fusion.9), channel_id=1, source_target_pairs={{0,16},{16,0},{1,17},{17,1},{2,18},{18,2},{3,19},{19,3},{4,20},{20... | collective-permute-start | bytes 6291464 | tf_op jit(solution)/shard_map/ppermute | solution.py:77
  1213.8 494.3 %reduce-scatter.14.cloned.1.call-start = ((), (), s32[]{:S(2)}) async-start(), calls=%async_computation.17 | async-start | bytes 8912896 | tf_op jit(solution)/shard_map/reduce_scatter | solution.py:65
  1475.5 60.9 %all-to-all-start.8 = ((bf16[16,64,1024]{2,1,0:T(8,128)(2,1)}), bf16[16,64,1024]{2,1,0:T(8,128)(2,1)}, u32[]{:S(2)}, u32[]{:S(2)}) async-start(bf16[16,64,1024]{2,1,0:T(8,128)(2,1)} %fusion.3), calls=%async_computation.12 | async-start | bytes 4194304 | tf_op jit(solution)/shard_map/all_to_all | solution.py:101
  1487.8 25.4 %collective-permute-start.6 = (bf16[256,2048]{1,0:T(8,128)(2,1)S(1)}, bf16[256,2048]{1,0:T(8,128)(2,1)S(1)}, u32[]{:S(2)}, u32[]{:S(2)}) collective-permute-start(bf16[256,2048]{1,0:T(8,128)(2,1)S(1)} %fusion.44), channel_id=1, source_target_pairs={{0,16},{16,0},{1,17},{17,1},{2,18},{18,2},{3,19},{19,3},{4,20},{20... | collective-permute-start | bytes 3145736 | tf_op jit(solution)/shard_map/ppermute | solution.py:77
  1513.4 24.6 %collective-permute-start.7 = (bf16[256,2048]{1,0:T(8,128)(2,1)S(1)}, bf16[256,2048]{1,0:T(8,128)(2,1)S(1)}, u32[]{:S(2)}, u32[]{:S(2)}) collective-permute-start(bf16[256,2048]{1,0:T(8,128)(2,1)S(1)} %fusion.10), channel_id=1, source_target_pairs={{0,16},{16,0},{1,17},{17,1},{2,18},{18,2},{3,19},{19,3},{4,20},{20... | collective-permute-start | bytes 3145736 | tf_op jit(solution)/shard_map/ppermute | solution.py:84
  1536.5 44.8 %collective-permute-start.5 = (bf16[16,64,1024]{2,1,0:T(8,128)(2,1)}, bf16[16,64,1024]{2,1,0:T(8,128)(2,1)}, u32[]{:S(2)}, u32[]{:S(2)}) collective-permute-start(bf16[16,64,1024]{2,1,0:T(8,128)(2,1)} %all-to-all-done.8), channel_id=1, source_target_pairs={{0,16},{16,0},{1,17},{17,1},{2,18},{18,2},{3,19},{19,3},{4,20},{20... | collective-permute-start | bytes 6291464 | tf_op jit(solution)/shard_map/ppermute | solution.py:84
  1555.6 44.5 %collective-permute-start = (bf16[16,64,384]{2,1,0:T(8,128)(2,1)}, bf16[16,64,384]{2,1,0:T(8,128)(2,1)}, u32[]{:S(2)}, u32[]{:S(2)}) collective-permute-start(bf16[16,64,384]{2,1,0:T(8,128)(2,1)} %fusion.49), channel_id=1, source_target_pairs={{0,16},{16,0},{1,17},{17,1},{2,18},{18,2},{3,19},{19,3},{4,20},{20... | collective-permute-start | bytes 2359304 | tf_op jit(solution)/shard_map/ppermute | solution.py:77
  1598.7 68.6 %collective-permute-start.2 = (bf16[64,2048]{1,0:T(8,128)(2,1)S(1)}, bf16[64,2048]{1,0:T(8,128)(2,1)}, u32[]{:S(2)}, u32[]{:S(2)}) collective-permute-start(bf16[64,2048]{1,0:T(8,128)(2,1)S(1)} %fusion.80), channel_id=1, source_target_pairs={{0,16},{16,0},{1,17},{17,1},{2,18},{18,2},{3,19},{19,3},{4,20},{20... | collective-permute-start | bytes 786440 | tf_op jit(solution)/shard_map/ppermute | solution.py:77
  1602.4 75.3 %all-to-all-start.7 = ((bf16[16,64,384]{2,1,0:T(8,128)(2,1)}), bf16[16,64,384]{2,1,0:T(8,128)(2,1)}, u32[]{:S(2)}, u32[]{:S(2)}) async-start(bf16[16,64,384]{2,1,0:T(8,128)(2,1)} %fusion.14), calls=%async_computation.11 | async-start | bytes 1572864 | tf_op jit(solution)/shard_map/all_to_all | solution.py:101
  1668.4 10.2 collective-permute-start.3
  1677.8 19.3 %collective-permute-start.1 = (bf16[16,64,384]{2,1,0:T(8,128)(2,1)}, bf16[16,64,384]{2,1,0:T(8,128)(2,1)S(1)}, u32[]{:S(2)}, u32[]{:S(2)}) collective-permute-start(bf16[16,64,384]{2,1,0:T(8,128)(2,1)} %all-to-all-done.7), channel_id=1, source_target_pairs={{0,16},{16,0},{1,17},{17,1},{2,18},{18,2},{3,19},{19,3},{4,20},{20... | collective-permute-start | bytes 2359304 | tf_op jit(solution)/shard_map/ppermute | solution.py:84
  (47 other events, 1405.0 us)
Sparse Core Ops, SparseCore 0:
  347.0 161.7 reduce-scatter.7
  712.2 135.2 reduce-scatter.9
  1063.1 104.5 reduce-scatter.11
  1213.9 135.5 reduce-scatter.15
  1470.6 130.2 reduce-scatter.13
